TPU v7x, 32 devices: a whole 2x2x4 slice. The times are simulated.
32 devices in a mesh: blk: 8 (over y, x, core), vec: 4 (over z).
Axes of the slice: x: 2, y: 2, z: 4, core: 2. Of those that a mesh axis runs over, the one named last changes fastest.
Arguments:
- trial: bfloat16 [64, 64, 4096], P('vec', None, 'blk'), may hold values from -0.01171875 to 0.01171875
- coupling: bfloat16 [8, 6, 512, 512], P('blk'), may hold values from -0.09375 to 0.09375
- partners: int32 [8, 6], P('blk'), may hold values from 0 to 7, as said below
- live: int32 [8], P('blk'), may hold values from 1 to 6, as said below
- diag_block: bfloat16 [4096, 512], P('blk'), may hold values from -0.25 to 0.25
- beta_coupling: bfloat16 [64, 64], replicated, may hold values from -0.75 to 0.75
- hdiag: float32 [64, 4096], P(None, 'blk'), may hold values from 0.5 to 4
Outputs:
- correction: bfloat16 [64, 64, 4096], P('vec', None, 'blk')
- subspace: float32 [64, 64], P(None, 'vec')
Inputs may be any that keep to these rules, and one draw needn't show every extreme that they name: `partners`: each row holds 6 different block numbers, none equal to the row's own block. `live`: some block uses all 6 slots in every draw.
All inputs are finite; a program needn't handle non-finite values.
Results may differ from a plain program's by a relative error of at most 0.0012.
Values may be sent and summed in bfloat16 or wider, within the bound.
A program may use at most 128 MiB of HBM per device.

v0:
```python
import jax
import jax.numpy as jnp
from jax import lax
from jax.sharding import PartitionSpec as P


def local(trial, coupling, partners, live, diag_block, beta_coupling, hdiag):
    root_count, beta_count, block_width = trial.shape
    row_count = root_count * beta_count
    contract = (((1,), (1,)), ((), ()))
    blocks = coupling[0]
    partner_ids = partners[0]
    live_count = live[0]
    flat = trial.reshape(row_count, block_width)
    sigma_flat = lax.dot_general(flat, diag_block, contract, preferred_element_type=jnp.float32)
    empty = jnp.zeros((row_count, block_width), jnp.float32)
    running = empty
    segment = lax.all_gather(trial, "blk", axis=2, tiled=True)
    span_width = segment.shape[2]
    seg_flat = segment.reshape(row_count, span_width)
    for member in range(blocks.shape[0]):
        relative = partner_ids[member] * block_width
        inside = (relative >= 0) & (relative + block_width <= span_width) & (member < live_count)
        start = jnp.clip(relative, 0, span_width - block_width)

        def multiply(total, start=start, member=member):
            piece = lax.dynamic_slice_in_dim(seg_flat, start, block_width, 1)
            return total + lax.dot_general(
                piece, blocks[member], contract, preferred_element_type=jnp.float32
            )

        def unchanged(total):
            return total

        running = lax.cond(inside, multiply, unchanged, running)
    trial_float = trial.astype(jnp.float32)
    beta_part = jnp.einsum("bc,kca->kba", beta_coupling, trial, preferred_element_type=jnp.float32)
    sigma = (
        (sigma_flat + running).reshape(root_count, beta_count, block_width)
        + beta_part
        + hdiag[None] * trial_float
    )
    all_roots = lax.all_gather(trial, "vec", axis=0, tiled=True)
    intersection_part = jnp.einsum(
        "kba,lba->kl", all_roots.astype(jnp.float32), sigma, precision=lax.Precision.HIGHEST
    )
    total_cells = beta_count * block_width * lax.axis_size("blk")
    theta_part = jnp.einsum("kba,kba->k", trial_float, sigma, precision=lax.Precision.HIGHEST)
    theta = lax.psum(theta_part, "blk")
    resid = sigma - theta[:, None, None] * trial_float
    gap = theta[:, None, None] - hdiag[None]
    raw = resid * gap / (gap * gap + 0.25)
    squares, subspace = lax.psum((jnp.sum(raw * raw, axis=(1, 2)), intersection_part), "blk")
    msq = squares / total_cells
    correction = (raw * lax.rsqrt(msq + 1e-06)[:, None, None]).astype(jnp.bfloat16)
    return (correction, subspace)


def solution(mesh):
    in_specs = (
        P("vec", None, "blk"),
        P("blk", None, None, None),
        P("blk", None),
        P("blk"),
        P("blk", None),
        P(),
        P(None, "blk"),
    )
    out_specs = (P("vec", None, "blk"), P(None, "vec"))
    return jax.shard_map(local, mesh=mesh, in_specs=in_specs, out_specs=out_specs, check_vma=False)
```

profile of v0, /device:TPU:0, one launch (start us, length us, event | category | flops | bytes accessed | tf_op | source)
XLA Modules:
  0.0 181.0 jit_solution(14991319289623215751)
XLA Ops:
  7.2 0.0 copy-start
  7.2 0.0 copy-start.5
  7.2 0.0 all-gather.3.cloned.1.call-start
  7.2 0.7 all-gather.3.cloned.1.call-update
  7.9 0.0 all-gather.5.cloned.1.call-start
  8.0 2.8 %copy.9 = bf16[16,64,512]{2,0,1:T(8,128)(2,1)} copy(bf16[16,64,512]{2,1,0:T(8,128)(2,1)} %param.19) | data formatting | bytes 2097152 | tf_op args[0]
  10.7 0.0 all-gather.5.cloned.1.call-update
  10.8 0.0 copy-done.5
  10.8 0.7 fusion.36
  16.1 52.4 %all-gather.3.cloned.1.call-done = bf16[16,64,4096]{2,1,0:T(8,128)(2,1)} async-done(((bf16[16,64,512]{2,1,0:T(8,128)(2,1)}), bf16[16,64,4096]{2,1,0:T(8,128)(2,1)}) %all-gather.3.cloned.1.call-update) | async-done | bytes 8388624 | tf_op jit(solution)/shard_map/all_gather | solution.py:18
  68.5 2.2 %conditional.6 = (f32[1024,512]{1,0:T(8,128)S(1)}) conditional(s32[]{:T(128)} %convert_element_type.30, () %tuple.44, (s32[1,1]{1,0:T(1,128)}, bf16[1024,4096]{1,0:T(8,128)(2,1)}, bf16[6,512,512]{2,1,0:T(8,128)(2,1)}, s32[1,1]{1,0:T(1,128)}, s32[1,1]{1,0:T(1,128)}) %tuple.81), branch_computations={%region_0.1_spmd, %region_1.2_spmd} | conditional | flops 536870912 | bytes 3670086 | solution.py:35
  68.5 2.2 %fusion = f32[1024,512]{1,0:T(8,128)S(1)} fusion(bf16[1024,4096]{1,0:T(8,128)(2,1)} %get-tuple-element.73, s32[]{:T(128)S(6)} %select_n.12, bf16[6,512,512]{2,1,0:T(8,128)(2,1)} %get-tuple-element.75), kind=kOutput, calls=%fused_computation | convolution fusion | flops 536870912 | bytes 3670020 | tf_op jit(solution)/shard_map/cond/branch_1_fun/dot_general | solution.py:28
  70.7 2.3 %conditional.7 = (f32[1024,512]{1,0:T(8,128)S(1)}) conditional(s32[]{:T(128)} %convert_element_type.29, f32[1024,512]{1,0:T(8,128)S(1)} %get-tuple-element.135, (s32[1,1]{1,0:T(1,128)}, bf16[1024,4096]{1,0:T(8,128)(2,1)}, bf16[6,512,512]{2,1,0:T(8,128)(2,1)}, f32[1024,512]{1,0:T(8,128)S(1)}, s32[1,1]{1,0:T(1,128)}, /*index=5*/s32[1,1]{1,0:T(1,128)}) %tuple.82), branch_computations={%region_2.3_spmd, %region_3.4_spmd} | conditional | flops 537395200 | bytes 5767238 | solution.py:35
  70.7 2.3 %convolution_add_fusion = f32[1024,512]{1,0:T(8,128)S(1)} fusion(f32[1024,512]{1,0:T(8,128)S(1)} %get-tuple-element.76, bf16[1024,4096]{1,0:T(8,128)(2,1)} %get-tuple-element.77, s32[]{:T(128)S(6)} %select_n.13, bf16[6,512,512]{2,1,0:T(8,128)(2,1)} %get-tuple-element.79), kind=kOutput, calls=%fused_computation.5 | convolution fusion | flops 537395200 | bytes 5767172 | tf_op jit(solution)/shard_map/cond/branch_1_fun/dot_general | solution.py:28
  73.0 2.3 %conditional.8 = (f32[1024,512]{1,0:T(8,128)S(1)}) conditional(s32[]{:T(128)} %convert_element_type.28, f32[1024,512]{1,0:T(8,128)S(1)} %get-tuple-element.136, (s32[1,1]{1,0:T(1,128)}, bf16[1024,4096]{1,0:T(8,128)(2,1)}, bf16[6,512,512]{2,1,0:T(8,128)(2,1)}, f32[1024,512]{1,0:T(8,128)S(1)}, s32[1,1]{1,0:T(1,128)}, /*index=5*/s32[1,1]{1,0:T(1,128)}) %tuple.83), branch_computations={%region_4.5_spmd, %region_5.6_spmd} | conditional | flops 537395200 | bytes 5767238 | solution.py:35
  73.0 2.3 %convolution_add_fusion.1 = f32[1024,512]{1,0:T(8,128)S(1)} fusion(f32[1024,512]{1,0:T(8,128)S(1)} %get-tuple-element.80, bf16[1024,4096]{1,0:T(8,128)(2,1)} %get-tuple-element.81, s32[]{:T(128)S(6)} %select_n.14, bf16[6,512,512]{2,1,0:T(8,128)(2,1)} %get-tuple-element.83), kind=kOutput, calls=%fused_computation.10 | convolution fusion | flops 537395200 | bytes 5767172 | tf_op jit(solution)/shard_map/cond/branch_1_fun/dot_general | solution.py:28
  75.4 0.0 copy-done
  75.4 0.0 copy-start.1
  75.4 0.0 copy-start.4
  75.4 0.0 copy-start.6
  75.4 2.1 %convolution_add_fusion.5 = f32[1024,512]{1,0:T(8,128)S(1)} fusion(f32[1024,512]{1,0:T(8,128)S(1)} %get-tuple-element.140, bf16[1024,512]{1,0:T(8,128)(2,1)} %bitcast.60, bf16[512,512]{1,0:T(8,128)(2,1)S(1)} %copy-done), kind=kOutput, calls=%fused_computation.44 | convolution fusion | flops 537395200 | bytes 5767168 | tf_op jit(solution)/shard_map/dot_general | solution.py:15
  77.5 0.0 copy-done.1
  77.5 0.0 copy-done.4
  77.5 0.0 copy-done.6
  77.5 0.0 copy-start.2
  77.5 2.0 %multiply_reduce_fusion = (f32[16]{0:T(128)S(1)}, f32[16,64,512]{2,1,0:T(8,128)}) fusion(bf16[16,64,512]{2,1,0:T(8,128)(2,1)S(1)} %copy-done.1, f32[64,512]{1,0:T(8,128)S(1)} %copy-done.4, f32[16,64,512]{2,1,0:T(8,128)S(1)} %bitcast.61, bf16[64,64]{1,0:T(8,128)(2,1)S(1)} %copy-done.6), kind=kOutput, calls=%fused_computation.39 | convolution fusion | flops 70778864 | bytes 5382208 | tf_op jit(solution)/shard_map/bc,kca->kba/dot_general | solution.py:37
  79.5 18.3 %psum.21 = f32[16]{0:T(128)S(1)} all-reduce(f32[16]{0:T(128)S(1)} %get-tuple-element.133), channel_id=1, replica_groups=mesh['blk'=8,'vec'=4] {'blk'}, use_global_device_ids=true, to_apply=%region_12.13 | all-reduce | flops 16 | bytes 128 | tf_op jit(solution)/shard_map/psum | solution.py:49
  97.9 0.0 copy-done.2
  97.9 3.8 %multiply_reduce_fusion.1 = (f32[16]{0:T(128)S(1)}, f32[16,64,512]{2,1,0:T(8,128)}) fusion(f32[64,512]{1,0:T(8,128)S(1)} %copy-done.4, f32[16,64,512]{2,1,0:T(8,128)} %get-tuple-element.134, bf16[16,64,512]{2,1,0:T(8,128)(2,1)S(1)} %copy-done.2, f32[16]{0:T(128)S(1)} %psum.21), kind=kLoop, calls=%fused_computation.43 | loop fusion | flops 5242864 | bytes 5374080 | tf_op jit(solution)/shard_map/reduce_sum | solution.py:53
  101.6 0.0 copy-start.3
  101.6 49.8 %all-gather.5.cloned.1.call-done = bf16[64,64,512]{2,0,1:T(8,128)(2,1)} async-done(((bf16[16,64,512]{2,0,1:T(8,128)(2,1)}), bf16[64,64,512]{2,0,1:T(8,128)(2,1)}) %all-gather.5.cloned.1.call-update) | async-done | bytes 4194320 | tf_op jit(solution)/shard_map/all_gather | solution.py:43
  151.4 6.8 %fusion.31 = f32[64,16]{0,1:T(8,128)S(1)} fusion(bf16[64,64,512]{2,0,1:T(8,128)(2,1)} %all-gather.5.cloned.1.call-done, f32[16,64,512]{2,1,0:T(8,128)} %get-tuple-element.134), kind=kOutput, calls=%fused_computation.45 | convolution fusion | flops 402653184 | bytes 6295552 | tf_op jit(solution)/shard_map/kba,lba->kl/dot_general | solution.py:44
  158.2 14.6 %all-reduce = (f32[16]{0:T(128)S(1)}, f32[64,16]{0,1:T(8,128)}) all-reduce(f32[16]{0:T(128)S(1)} %get-tuple-element.125, f32[64,16]{0,1:T(8,128)S(1)} %fusion.31), channel_id=1, replica_groups=mesh['blk'=8,'vec'=4] {'blk'}, use_global_device_ids=true, to_apply=%region_14.15 | all-reduce | flops 1040 | bytes 8320 | tf_op jit(solution)/shard_map/psum | solution.py:53
  172.8 0.0 copy-done.3
  172.8 1.3 multiply_convert_fusion
  (4 shorter events, 0.0 us)
Async XLA Ops:
  7.2 68.2 %copy-start = (bf16[512,512]{1,0:T(8,128)(2,1)S(1)}, bf16[512,512]{1,0:T(8,128)(2,1)}, u32[]{:S(2)}) copy-start(bf16[512,512]{1,0:T(8,128)(2,1)} %param.23) | copy-start | bytes 1572868
  7.2 3.6 %copy-start.5 = (s32[1,6]{1,0:T(1,128)S(1)}, s32[1,6]{1,0:T(1,128)}, u32[]{:S(2)}) copy-start(s32[1,6]{1,0:T(1,128)} %param.21) | copy-start | bytes 76
  7.2 61.3 %all-gather.3.cloned.1.call-start = ((), (), s32[]{:S(2)}) async-start(), calls=%async_computation | async-start | bytes 9437184 | tf_op jit(solution)/shard_map/all_gather | solution.py:18
  7.9 143.5 %all-gather.5.cloned.1.call-start = ((), (), s32[]{:S(2)}) async-start(), calls=%async_computation.1 | async-start | bytes 5242880 | tf_op jit(solution)/shard_map/all_gather | solution.py:43
  75.4 2.1 %copy-start.1 = (bf16[16,64,512]{2,1,0:T(8,128)(2,1)S(1)}, bf16[16,64,512]{2,1,0:T(8,128)(2,1)}, u32[]{:S(2)}) copy-start(bf16[16,64,512]{2,1,0:T(8,128)(2,1)} %param.19) | copy-start | bytes 3145732
  75.4 2.1 %copy-start.4 = (f32[64,512]{1,0:T(8,128)S(1)}, f32[64,512]{1,0:T(8,128)}, u32[]{:S(2)}) copy-start(f32[64,512]{1,0:T(8,128)} %param.25) | copy-start | bytes 393220
  75.4 2.1 %copy-start.6 = (bf16[64,64]{1,0:T(8,128)(2,1)S(1)}, bf16[64,64]{1,0:T(8,128)(2,1)}, u32[]{:S(2)}) copy-start(bf16[64,64]{1,0:T(8,128)(2,1)} %param.24) | copy-start | bytes 24580
  77.5 20.4 %copy-start.2 = (bf16[16,64,512]{2,1,0:T(8,128)(2,1)S(1)}, bf16[16,64,512]{2,1,0:T(8,128)(2,1)}, u32[]{:S(2)}) copy-start(bf16[16,64,512]{2,1,0:T(8,128)(2,1)} %param.19) | copy-start | bytes 3145732
  101.6 71.2 %copy-start.3 = (f32[16,64,512]{2,1,0:T(8,128)S(1)}, f32[16,64,512]{2,1,0:T(8,128)}, u32[]{:S(2)}) copy-start(f32[16,64,512]{2,1,0:T(8,128)} %get-tuple-element.126) | copy-start | bytes 6291460
Sparse Core Ops, SparseCore 0:
  9.9 58.5 all-gather.2
  70.6 80.7 all-gather.4
where the time goes:
time: 181 us
  waiting for transfers between devices  103 us (57%)
  blocking collectives  32.9 us (18%)
  between operations  18.8 us (10%)
  matrix products  17.6 us (10%)
  other arithmetic  5.06 us (3%)
  local copies, waits for them, and re-layouts  3.5 us (2%)
    all_gather x1, waiting for transfers between devices, local(): segment = lax.all_gather(trial, 'blk', axis=2, tiled=True)  52.4 us
    all_gather x1, waiting for transfers between devices, local(): all_roots = lax.all_gather(trial, 'vec', axis=0, tiled=True)  49.8 us
    psum x1, blocking collectives, local(): theta = lax.psum(theta_part, 'blk')  18.3 us
    psum x1, blocking collectives, local(): lax.psum((jnp.sum(raw * raw, axis=(1, 2)), intersection_part), 'blk')  14.6 us
    dot_general x1, matrix products, local(): jnp.einsum('kba,lba->kl', all_roots.astype(jnp.float32), sigma, precision...  6.82 us
    dot_general x3, matrix products, multiply(): lax.dot_general(piece, blocks[member], contract, preferred_element_type=j...  6.74 us
    reduce_sum x1, other arithmetic, local(): jnp.sum(raw * raw, axis=(1, 2))  3.75 us
  transfers between devices with their start and end apart: 2, of which 2 were waited for; matrix products, arithmetic and copies ran while one was open for 10% of the time, Pallas kernels for 0%

commit v1 on v0

--- a/solution.py
+++ b/solution.py
@@ -1,10 +1,14 @@
+import functools
+
 import jax
 import jax.numpy as jnp
 from jax import lax
+from jax.experimental import pallas as pl
+from jax.experimental.pallas import tpu as pltpu
 from jax.sharding import PartitionSpec as P
 
 
-def local(trial, coupling, partners, live, diag_block, beta_coupling, hdiag):
+def gathered(trial, coupling, partners, live, diag_block, beta_coupling, hdiag):
     root_count, beta_count, block_width = trial.shape
     row_count = root_count * beta_count
     contract = (((1,), (1,)), ((), ()))
@@ -56,7 +60,409 @@
     return (correction, subspace)
 
 
+CHUNKS = 4
+MESH = pl.DeviceIdType.MESH
+CONTRACT = (((1,), (1,)), ((), ()))
+
+
+def kernel(
+    depth, partners, live, trial, coupling, diag, beta, hdiag, correction, subspace,
+    held, weights, slots, roots, sigma, rounded, edge, rows, stats, products, theta, totals, edge_total,
+    load_sem, blk_send, blk_recv, vec_send, vec_recv, stat_send, stat_recv, edge_send, edge_recv,
+):
+    me, z = lax.axis_index("blk"), lax.axis_index("vec")
+    root_count, beta_count, width = trial.shape
+    piece = beta_count // CHUNKS
+    cells = root_count * piece
+    last = CHUNKS - 1
+    members = held.shape[0]
+    core, x, y = me % 2, (me // 2) % 2, me // 4
+    is_end = (z == 0) | (z == depth - 1)
+    mate = z + 1 - 2 * (z % 2)
+
+    def peer(r):
+        flip = lambda bit, on: 1 - bit if on else bit
+        return flip(y, r & 4) * 4 + flip(x, r & 2) * 2 + flip(core, r & 1)
+
+    def part(ref, c):
+        return ref.at[:, pl.ds(c * piece, piece), :]
+
+    def remote(src, dst, send, recv, device):
+        return pltpu.make_async_remote_copy(
+            src_ref=src, dst_ref=dst, send_sem=send, recv_sem=recv, device_id=device, device_id_type=MESH
+        )
+
+    loads = [
+        pltpu.make_async_copy(trial, held.at[0], load_sem.at[0]),
+        pltpu.make_async_copy(diag, weights.at[0], load_sem.at[1]),
+        pltpu.make_async_copy(coupling.at[0], slots, load_sem.at[2]),
+        pltpu.make_async_copy(trial, roots.at[z], load_sem.at[3]),
+    ]
+    for load in loads:
+        load.start()
+
+    barrier = pltpu.get_barrier_semaphore()
+    for r in range(1, members):
+        pl.semaphore_signal(barrier, inc=1, device_id={"blk": peer(r)}, device_id_type=MESH)
+
+    @pl.when(z < depth - 1)
+    def _():
+        pl.semaphore_signal(barrier, inc=1, device_id={"vec": z + 1}, device_id_type=MESH)
+
+    @pl.when(z > 0)
+    def _():
+        pl.semaphore_signal(barrier, inc=1, device_id={"vec": z - 1}, device_id_type=MESH)
+
+    pl.semaphore_wait(barrier, members + 1 - is_end.astype(jnp.int32))
+
+    def blk_copy(r, hop, c):
+        src = trial if r == 0 else held.at[r]
+        return remote(
+            part(src, c), part(held.at[r ^ hop], c), blk_send.at[r ^ hop, c], blk_recv.at[r ^ hop, c],
+            {"blk": peer(hop)},
+        )
+
+    sent = []
+
+    def blk_start(r, hop, c):
+        copy = blk_copy(r, hop, c)
+        copy.start()
+        sent.append(copy)
+
+    def blk_wait(slot, c):
+        blk_copy(0, slot, c).wait_recv()
+
+    def vec_copy(origin, side, c, src):
+        return remote(
+            part(src, c), part(roots.at[origin], c), vec_send.at[side, origin, c], vec_recv.at[origin, c],
+            {"vec": z + 1 - 2 * side},
+        )
+
+    def goes(side, c):
+        limit = 2 if c == last else 1
+        return (z < depth - limit) if side == 0 else (z >= limit)
+
+    def has(step, side, c):
+        origin = z - step if side == 0 else z + step
+        there = (origin >= 0) & (origin < depth)
+        if c == last:
+            there = there & jnp.logical_not(is_end)
+        return there, origin
+
+    for c in range(CHUNKS):
+        blk_start(0, 2, c)
+        blk_start(0, 4, (c + 2) % CHUNKS)
+        blk_start(0, 1, c)
+        for side in (0, 1):
+            @pl.when(goes(side, c))
+            def _():
+                vec_copy(z, side, c, trial).start()
+
+    def vec_step(step, c):
+        for side in (0, 1):
+            there, origin = has(step, side, c)
+
+            @pl.when(there)
+            def _():
+                vec_copy(origin, side, c, trial).wait_recv()
+
+            @pl.when(there & goes(side, c))
+            def _():
+                vec_copy(origin, side, c, roots.at[origin]).start()
+
+    for load in loads:
+        load.wait()
+
+    def select(r):
+        block = peer(r)
+        index, hit = jnp.int32(0), jnp.float32(0.0)
+        for c in range(slots.shape[0]):
+            match = (partners[0, c] == block) & (c < live[0])
+            index = jnp.where(match, c, index)
+            hit = jnp.where(match, jnp.float32(1.0), hit)
+        weights[r] = (slots[index].astype(jnp.float32) * hit).astype(weights.dtype)
+
+    for r in range(1, members):
+        select(r)
+
+    def own(k, _):
+        vectors = held[0, k]
+        sigma[k] = (
+            jnp.dot(beta[...], vectors, preferred_element_type=jnp.float32)
+            + hdiag[...] * vectors.astype(jnp.float32)
+        )
+        return 0
+
+    lax.fori_loop(0, root_count, own, 0)
+
+    def multiply(r, c):
+        span = pl.ds(pl.multiple_of(c * piece, piece), piece)
+        left = held[r, :, span, :].reshape(cells, width)
+        out = lax.dot_general(left, weights[r], CONTRACT, preferred_element_type=jnp.float32)
+        sigma[:, span, :] += out.reshape(root_count, piece, width)
+
+    def multiply_all(first, count):
+        def body(i, _):
+            multiply(first + i // CHUNKS, i % CHUNKS)
+            return 0
+
+        lax.fori_loop(0, count * CHUNKS, body, 0)
+
+    for c in range(CHUNKS):
+        blk_wait(1, c)
+    multiply_all(0, 2)
+    products[...] = jnp.zeros_like(products)
+
+    for t in range(CHUNKS):
+        u = (t + 2) % CHUNKS
+        blk_wait(2, t)
+        if t < 2:
+            blk_start(2, 4, t)
+        blk_start(2, 1, t)
+        blk_wait(4, u)
+        if t < 2:
+            blk_start(4, 2, u)
+        blk_start(4, 1, u)
+        vec_step(1, t)
+    for c in range(CHUNKS):
+        blk_wait(3, c)
+        blk_wait(5, c)
+    multiply_all(2, 4)
+    for t in range(2):
+        for c in (t, t + 2):
+            blk_wait(6, c)
+            blk_start(6, 1, c)
+        vec_step(2, t)
+        for c in (t, t + 2):
+            blk_wait(7, c)
+
+        def tail(i, _, t=t):
+            multiply(6 + i // 2, t + 2 * (i % 2))
+            return 0
+
+        lax.fori_loop(0, 4, tail, 0)
+
+    def share(phase):
+        for r in range(1, members):
+            place = stats.at[phase, me]
+            remote(place, place, stat_send.at[phase, r], stat_recv.at[phase, me], {"blk": peer(r)}).start()
+
+    def gather(phase):
+        for r in range(1, members):
+            place = stats.at[phase, peer(r)]
+            remote(place, place, stat_send.at[phase, r], stat_recv.at[phase, peer(r)], {"blk": peer(r)}).wait_recv()
+        total = stats[phase, 0]
+        for j in range(1, members):
+            total = total + stats[phase, j]
+        return total
+
+    def finish(k, _):
+        value = sigma[k]
+        rounded[k] = value.astype(rounded.dtype)
+        rows[pl.ds(k, 1), :] = jnp.sum(value * held[0, k].astype(jnp.float32), axis=0, keepdims=True)
+        return 0
+
+    lax.fori_loop(0, root_count, finish, 0)
+    stats[0, me] = jnp.broadcast_to(jnp.sum(rows[...], axis=1, keepdims=True), stats.shape[2:])
+    share(0)
+
+    def edge_copy():
+        return remote(part(rounded, last), edge, edge_send.at[0], edge_recv.at[0], {"vec": mate})
+
+    def total_copy():
+        return remote(edge_total.at[0], edge_total.at[1], edge_send.at[1], edge_recv.at[1], {"vec": mate})
+
+    @pl.when(is_end)
+    def _():
+        edge_copy().start()
+
+    row = lax.broadcasted_iota(jnp.int32, (cells, cells), 0) % piece
+    column = lax.broadcasted_iota(jnp.int32, (cells, cells), 1) % piece
+    same = (row == column).astype(jnp.float32)
+
+    def product(which, origin, c, right):
+        span = pl.ds(pl.multiple_of(c * piece, piece), piece)
+        left = roots[origin, :, span, :].reshape(cells, width)
+        out = lax.dot_general(left, right.reshape(cells, width), CONTRACT, preferred_element_type=jnp.float32)
+        out = jnp.sum((out * same).reshape(root_count, piece, cells), axis=1)
+        place = pl.ds(pl.multiple_of(origin * root_count, root_count), root_count)
+        products[which, place, :] += out
+
+    def products_of(origin, start, stop):
+        def body(c, _):
+            span = pl.ds(pl.multiple_of(c * piece, piece), piece)
+            product(0, origin, c, rounded[:, span, :])
+            return 0
+
+        lax.fori_loop(start, stop, body, 0)
+
+    def products_at(step, start, stop):
+        for side in (0, 1):
+            for low, high in ((start, min(stop, last)), (max(start, last), stop)):
+                if low < high:
+                    there, origin = has(step, side, low)
+
+                    @pl.when(there)
+                    def _():
+                        products_of(origin, low, high)
+
+    products_of(z, 0, last)
+
+    @pl.when(jnp.logical_not(is_end))
+    def _():
+        products_of(z, last, CHUNKS)
+
+    products_at(1, 0, CHUNKS)
+
+    theta[...] = jnp.broadcast_to(gather(0)[:, :1], theta.shape)
+
+    def residual(k, _):
+        value = theta[pl.ds(k, 1), :]
+        resid = sigma[k] - value * held[0, k].astype(jnp.float32)
+        gap = value - hdiag[...]
+        raw = resid * gap / (gap * gap + 0.25)
+        sigma[k] = raw
+        rows[pl.ds(k, 1), :] = jnp.sum(raw * raw, axis=0, keepdims=True)
+        return 0
+
+    lax.fori_loop(0, root_count, residual, 0)
+    stats[1, me] = jnp.broadcast_to(jnp.sum(rows[...], axis=1, keepdims=True), stats.shape[2:])
+    share(1)
+    vec_step(2, 2)
+    products_at(2, 0, last)
+    msq = gather(1) / (beta_count * width * members)
+    theta[...] = jnp.broadcast_to(lax.rsqrt(msq + 1e-06)[:, :1], theta.shape)
+
+    def scale(k, _):
+        correction[k] = (sigma[k] * theta[pl.ds(k, 1), :]).astype(correction.dtype)
+        return 0
+
+    lax.fori_loop(0, root_count, scale, 0)
+
+    pick = (
+        lax.broadcasted_iota(jnp.int32, (root_count, cells), 1) // piece
+        == lax.broadcasted_iota(jnp.int32, (root_count, cells), 0)
+    ).astype(jnp.float32)
+
+    def collect(which):
+        return lax.dot_general(
+            pick, products[which], CONTRACT, precision=lax.Precision.HIGHEST, preferred_element_type=jnp.float32
+        )
+
+    vec_step(2, last)
+    products_at(2, last, CHUNKS)
+
+    @pl.when(jnp.logical_not(is_end))
+    def _():
+        edge_copy().wait_recv()
+
+        def body(origin, _):
+            product(1, origin, last, edge[...])
+            return 0
+
+        lax.fori_loop(0, depth, body, 0)
+        edge_total[0] = collect(1)
+        total_copy().start()
+
+    for c in range(last):
+        vec_step(3, c)
+        products_at(3, c, c + 1)
+    totals[...] = collect(0)
+
+    @pl.when(is_end)
+    def _():
+        total_copy().wait_recv()
+        totals[...] += edge_total[1]
+
+    stats[2, me] = totals[...]
+    share(2)
+
+    for copy in sent:
+        copy.wait_send()
+    for side in (0, 1):
+        for c in range(CHUNKS):
+            @pl.when(goes(side, c))
+            def _():
+                vec_copy(z, side, c, trial).wait_send()
+
+            for step in range(1, depth):
+                there, origin = has(step, side, c)
+
+                @pl.when(there & goes(side, c))
+                def _():
+                    vec_copy(origin, side, c, trial).wait_send()
+
+    @pl.when(is_end)
+    def _():
+        edge_copy().wait_send()
+
+    @pl.when(jnp.logical_not(is_end))
+    def _():
+        total_copy().wait_send()
+
+    subspace[...] = gather(2)
+    for phase in range(3):
+        for r in range(1, members):
+            place = stats.at[phase, me]
+            remote(place, place, stat_send.at[phase, r], stat_recv.at[phase, me], {"blk": peer(r)}).wait_send()
+
+
+def exchanged(depth, members, trial, coupling, partners, live, diag_block, beta_coupling, hdiag):
+    root_count, beta_count, width = trial.shape
+    slot_count = coupling.shape[1]
+    cells = root_count * (beta_count // CHUNKS)
+    lanes = 128
+    kind, full = trial.dtype, jnp.float32
+    vmem, smem, anywhere = (
+        pl.BlockSpec(memory_space=pltpu.VMEM),
+        pl.BlockSpec(memory_space=pltpu.SMEM),
+        pl.BlockSpec(memory_space=pl.ANY),
+    )
+    dma = pltpu.SemaphoreType.DMA
+    correction, subspace = pl.pallas_call(
+        functools.partial(kernel, depth),
+        out_shape=(
+            jax.ShapeDtypeStruct(trial.shape, kind),
+            jax.ShapeDtypeStruct((root_count, lanes), full),
+        ),
+        in_specs=[smem, smem, anywhere, anywhere, anywhere, vmem, vmem],
+        out_specs=(vmem, vmem),
+        scratch_shapes=[
+            pltpu.VMEM((members,) + trial.shape, kind),
+            pltpu.VMEM((members, width, width), kind),
+            pltpu.VMEM((slot_count, width, width), kind),
+            pltpu.VMEM((depth,) + trial.shape, kind),
+            pltpu.VMEM(trial.shape, full),
+            pltpu.VMEM(trial.shape, kind),
+            pltpu.VMEM((root_count, beta_count // CHUNKS, width), kind),
+            pltpu.VMEM((root_count, width), full),
+            pltpu.VMEM((3, members, root_count, lanes), full),
+            pltpu.VMEM((2, lanes, cells), full),
+            pltpu.VMEM((root_count, width), full),
+            pltpu.VMEM((root_count, lanes), full),
+            pltpu.VMEM((2, root_count, lanes), full),
+            dma((4,)),
+            dma((members, CHUNKS)),
+            dma((members, CHUNKS)),
+            dma((2, depth, CHUNKS)),
+            dma((depth, CHUNKS)),
+            dma((3, members)),
+            dma((3, members)),
+            dma((2,)),
+            dma((2,)),
+        ],
+        compiler_params=pltpu.CompilerParams(collective_id=0, has_side_effects=True, vmem_limit_bytes=50 * 2**20),
+        name="davidson",
+    )(partners, live, trial, coupling, diag_block, beta_coupling, hdiag)
+    return correction, subspace[:, : root_count * depth].T
+
+
 def solution(mesh):
+    depth, members = mesh.shape["vec"], mesh.shape["blk"]
+    if depth == 4 and members == 8:
+        local = functools.partial(exchanged, depth, members)
+    else:
+        local = gathered
     in_specs = (
         P("vec", None, "blk"),
         P("blk", None, None, None),

time: 181 us -> 70.5 us (0.39)
  waiting for transfers between devices: 103 us -> 0 us
  Pallas kernels: 0 us -> 62.8 us
  blocking collectives: 32.9 us -> 0 us
  matrix products: 17.6 us -> 0 us
  between operations: 18.8 us -> 1.3 us
  other arithmetic: 5.06 us -> 0 us
  local copies, waits for them, and re-layouts: 3.5 us -> 6.1 us
    all_gather x2 -> x0, waiting for transfers between devices: 102 us -> none  [the longest x1 52.4 us: local(): segment = lax.all_gather(trial, 'blk', axis=2, tiled=True)]
    pallas_call x0 -> x1, Pallas kernels: none -> 62.8 us  [exchanged(): pl.pallas_call(functools.partial(kernel, depth), out_shape=(jax.ShapeDtyp...]
    psum x2 -> x0, blocking collectives: 32.9 us -> none  [the longest x1 18.3 us: local(): theta = lax.psum(theta_part, 'blk')]
    dot_general x6 -> x0, matrix products: 17.6 us -> none  [the longest x1 6.82 us: local(): jnp.einsum('kba,lba->kl', all_roots.astype(jnp.float32), sigma, precision...]
    reduce_sum x1 -> x0, other arithmetic: 3.75 us -> none  [local(): jnp.sum(raw * raw, axis=(1, 2))]
    unnamed x15 -> x11, local copies, waits for them, and re-layouts: 2.82 us -> 5.5 us
  transfers between devices with their start and end apart: 2 -> 0, of which waited for: 2 -> 0; matrix products, arithmetic and copies ran while one was open for 10% -> 0% of each run, Pallas kernels for 0% -> 0%
where the time goes in v1:
time: 70.5 us; the launch traced here: 70.2 us
  Pallas kernels  62.8 us (89%)
  local copies, waits for them, and re-layouts  6.1 us (9%)
  between operations  1.3 us (2%)
    pallas_call x1, Pallas kernels, exchanged(): pl.pallas_call(functools.partial(kernel, depth), out_shape=(jax.ShapeDtyp...  62.8 us
    unnamed x11, local copies, waits for them, and re-layouts  5.5 us

profile of v1, /device:TPU:0, one launch (start us, length us, event | category | flops | bytes accessed | tf_op | source)
XLA Modules:
  0.0 70.2 jit_solution(10224272019633324036)
XLA Ops:
  1.3 0.0 copy-start
  1.3 1.2 %copy-done = bf16[16,64,512]{2,1,0:T(8,128)(2,1)S(1)} copy-done((bf16[16,64,512]{2,1,0:T(8,128)(2,1)S(1)}, bf16[16,64,512]{2,1,0:T(8,128)(2,1)}, u32[]{:S(2)}) %copy-start) | copy-done | bytes 1048600
  2.5 0.0 copy-start.1
  2.5 1.0 %copy-done.1 = bf16[512,512]{1,0:T(8,128)(2,1)S(1)} copy-done((bf16[512,512]{1,0:T(8,128)(2,1)S(1)}, bf16[512,512]{1,0:T(8,128)(2,1)}, u32[]{:S(2)}) %copy-start.1) | copy-done | bytes 524312
  3.5 0.0 copy-start.2
  3.5 0.9 %copy-done.2 = f32[64,512]{1,0:T(8,128)S(1)} copy-done((f32[64,512]{1,0:T(8,128)S(1)}, f32[64,512]{1,0:T(8,128)}, u32[]{:S(2)}) %copy-start.2) | copy-done | bytes 131096
  4.4 0.0 copy-start.3
  4.5 0.7 %copy-done.3 = bf16[64,64]{1,0:T(8,128)(2,1)S(1)} copy-done((bf16[64,64]{1,0:T(8,128)(2,1)S(1)}, bf16[64,64]{1,0:T(8,128)(2,1)}, u32[]{:S(2)}) %copy-start.3) | copy-done | bytes 8216
  5.2 0.0 copy-start.4
  5.2 0.7 copy-done.4
  5.8 62.8 %davidson.1 = (bf16[16,64,512]{2,1,0:T(8,128)(2,1)S(1)}, f32[16,128]{1,0:T(8,128)S(1)}) custom-call(s32[1,6]{1,0:T(1,128)S(1)} %copy-done.4, s32[1]{0:T(128)S(6)} %copy.10.live, bf16[16,64,512]{2,1,0:T(8,128)(2,1)S(1)} %copy-done, bf16[1,6,512,512]{3,2,1,0:T(8,128)(2,1)} %coupling.1, bf16[512,512]{1,0:T(8,128)(2,1)S(1)} %copy-done.1, ...), custom_call_target="tpu_custom_call" | custom-call | tf_op jit(solution)/shard_map/davidson/pallas_call | solution.py:422
  68.6 0.6 slice_bitcast_fusion
  69.2 1.0 %copy.11 = bf16[16,64,512]{2,1,0:T(8,128)(2,1)} copy(bf16[16,64,512]{2,1,0:T(8,128)(2,1)S(1)} %get-tuple-element.8) | data formatting | bytes 2097152
Async XLA Ops:
  1.3 1.2 %copy-start = (bf16[16,64,512]{2,1,0:T(8,128)(2,1)S(1)}, bf16[16,64,512]{2,1,0:T(8,128)(2,1)}, u32[]{:S(2)}) copy-start(bf16[16,64,512]{2,1,0:T(8,128)(2,1)} %trial.1) | copy-start | bytes 3145732
  2.5 1.0 %copy-start.1 = (bf16[512,512]{1,0:T(8,128)(2,1)S(1)}, bf16[512,512]{1,0:T(8,128)(2,1)}, u32[]{:S(2)}) copy-start(bf16[512,512]{1,0:T(8,128)(2,1)} %diag.1) | copy-start | bytes 1572868
  3.5 0.9 %copy-start.2 = (f32[64,512]{1,0:T(8,128)S(1)}, f32[64,512]{1,0:T(8,128)}, u32[]{:S(2)}) copy-start(f32[64,512]{1,0:T(8,128)} %hdiag.1) | copy-start | bytes 393220
  4.4 0.7 %copy-start.3 = (bf16[64,64]{1,0:T(8,128)(2,1)S(1)}, bf16[64,64]{1,0:T(8,128)(2,1)}, u32[]{:S(2)}) copy-start(bf16[64,64]{1,0:T(8,128)(2,1)} %beta.1) | copy-start | bytes 24580
  5.2 0.7 copy-start.4

commit v2 on v1

--- a/solution.py
+++ b/solution.py
@@ -66,8 +66,8 @@
 
 
 def kernel(
-    depth, partners, live, trial, coupling, diag, beta, hdiag, correction, subspace,
-    held, weights, slots, roots, sigma, rounded, edge, rows, stats, products, theta, totals, edge_total,
+    depth, partners_in, live, trial, coupling, diag, beta_in, hdiag_in, correction, subspace,
+    partners, beta, hdiag, held, weights, slots, roots, sigma, rounded, edge, rows, stats, products, theta, totals, edge_total,
     load_sem, blk_send, blk_recv, vec_send, vec_recv, stat_send, stat_recv, edge_send, edge_recv,
 ):
     me, z = lax.axis_index("blk"), lax.axis_index("vec")
@@ -97,6 +97,9 @@
         pltpu.make_async_copy(diag, weights.at[0], load_sem.at[1]),
         pltpu.make_async_copy(coupling.at[0], slots, load_sem.at[2]),
         pltpu.make_async_copy(trial, roots.at[z], load_sem.at[3]),
+        pltpu.make_async_copy(partners_in, partners, load_sem.at[4]),
+        pltpu.make_async_copy(beta_in, beta, load_sem.at[5]),
+        pltpu.make_async_copy(hdiag_in, hdiag, load_sem.at[6]),
     ]
     for load in loads:
         load.start()
@@ -313,6 +316,8 @@
         products_of(z, last, CHUNKS)
 
     products_at(1, 0, CHUNKS)
+    vec_step(2, 2)
+    products_at(2, 0, last)
 
     theta[...] = jnp.broadcast_to(gather(0)[:, :1], theta.shape)
 
@@ -328,8 +333,6 @@
     lax.fori_loop(0, root_count, residual, 0)
     stats[1, me] = jnp.broadcast_to(jnp.sum(rows[...], axis=1, keepdims=True), stats.shape[2:])
     share(1)
-    vec_step(2, 2)
-    products_at(2, 0, last)
     msq = gather(1) / (beta_count * width * members)
     theta[...] = jnp.broadcast_to(lax.rsqrt(msq + 1e-06)[:, :1], theta.shape)
 
@@ -416,7 +419,7 @@
     vmem, smem, anywhere = (
         pl.BlockSpec(memory_space=pltpu.VMEM),
         pl.BlockSpec(memory_space=pltpu.SMEM),
-        pl.BlockSpec(memory_space=pl.ANY),
+        pl.BlockSpec(memory_space=pltpu.HBM),
     )
     dma = pltpu.SemaphoreType.DMA
     correction, subspace = pl.pallas_call(
@@ -425,9 +428,12 @@
             jax.ShapeDtypeStruct(trial.shape, kind),
             jax.ShapeDtypeStruct((root_count, lanes), full),
         ),
-        in_specs=[smem, smem, anywhere, anywhere, anywhere, vmem, vmem],
+        in_specs=[anywhere, smem] + [anywhere] * 5,
         out_specs=(vmem, vmem),
         scratch_shapes=[
+            pltpu.SMEM(partners.shape, partners.dtype),
+            pltpu.VMEM(beta_coupling.shape, beta_coupling.dtype),
+            pltpu.VMEM(hdiag.shape, hdiag.dtype),
             pltpu.VMEM((members,) + trial.shape, kind),
             pltpu.VMEM((members, width, width), kind),
             pltpu.VMEM((slot_count, width, width), kind),
@@ -441,7 +447,7 @@
             pltpu.VMEM((root_count, width), full),
             pltpu.VMEM((root_count, lanes), full),
             pltpu.VMEM((2, root_count, lanes), full),
-            dma((4,)),
+            dma((7,)),
             dma((members, CHUNKS)),
             dma((members, CHUNKS)),
             dma((2, depth, CHUNKS)),

time: 70.5 us -> 70.1 us (level)
  no operation moved by 1% of the time
where the time goes in v2:
time: 70.1 us; the launch traced here: 69.9 us
  Pallas kernels  62.5 us (89%)
  local copies, waits for them, and re-layouts  6.1 us (9%)
  between operations  1.3 us (2%)
    pallas_call x1, Pallas kernels, exchanged(): pl.pallas_call(functools.partial(kernel, depth), out_shape=(jax.ShapeDtyp...  62.5 us
    unnamed x11, local copies, waits for them, and re-layouts  5.5 us

profile of v2, /device:TPU:0, one launch (start us, length us, event | category | flops | bytes accessed | tf_op | source)
XLA Modules:
  0.0 69.9 jit_solution(12819027258555960001)
XLA Ops:
  1.3 0.0 copy-start
  1.3 1.2 %copy-done = bf16[16,64,512]{2,1,0:T(8,128)(2,1)S(1)} copy-done((bf16[16,64,512]{2,1,0:T(8,128)(2,1)S(1)}, bf16[16,64,512]{2,1,0:T(8,128)(2,1)}, u32[]{:S(2)}) %copy-start) | copy-done | bytes 1048600
  2.5 0.0 copy-start.1
  2.5 1.0 %copy-done.1 = bf16[512,512]{1,0:T(8,128)(2,1)S(1)} copy-done((bf16[512,512]{1,0:T(8,128)(2,1)S(1)}, bf16[512,512]{1,0:T(8,128)(2,1)}, u32[]{:S(2)}) %copy-start.1) | copy-done | bytes 524312
  3.5 0.0 copy-start.2
  3.5 0.9 %copy-done.2 = f32[64,512]{1,0:T(8,128)S(1)} copy-done((f32[64,512]{1,0:T(8,128)S(1)}, f32[64,512]{1,0:T(8,128)}, u32[]{:S(2)}) %copy-start.2) | copy-done | bytes 131096
  4.4 0.0 copy-start.3
  4.5 0.7 %copy-done.3 = bf16[64,64]{1,0:T(8,128)(2,1)S(1)} copy-done((bf16[64,64]{1,0:T(8,128)(2,1)S(1)}, bf16[64,64]{1,0:T(8,128)(2,1)}, u32[]{:S(2)}) %copy-start.3) | copy-done | bytes 8216
  5.2 0.0 copy-start.4
  5.2 0.7 copy-done.4
  5.8 62.5 %davidson.1 = (bf16[16,64,512]{2,1,0:T(8,128)(2,1)S(1)}, f32[16,128]{1,0:T(8,128)S(1)}) custom-call(s32[1,6]{1,0:T(1,128)S(1)} %copy-done.4, s32[1]{0:T(128)S(6)} %copy.10.live, bf16[16,64,512]{2,1,0:T(8,128)(2,1)S(1)} %copy-done, bf16[1,6,512,512]{3,2,1,0:T(8,128)(2,1)} %coupling.1, bf16[512,512]{1,0:T(8,128)(2,1)S(1)} %copy-done.1, ...), custom_call_target="tpu_custom_call" | custom-call | tf_op jit(solution)/shard_map/davidson/pallas_call | solution.py:425
  68.3 0.6 slice_bitcast_fusion
  68.9 1.0 %copy.11 = bf16[16,64,512]{2,1,0:T(8,128)(2,1)} copy(bf16[16,64,512]{2,1,0:T(8,128)(2,1)S(1)} %get-tuple-element.8) | data formatting | bytes 2097152
Async XLA Ops:
  1.3 1.2 %copy-start = (bf16[16,64,512]{2,1,0:T(8,128)(2,1)S(1)}, bf16[16,64,512]{2,1,0:T(8,128)(2,1)}, u32[]{:S(2)}) copy-start(bf16[16,64,512]{2,1,0:T(8,128)(2,1)} %trial.1) | copy-start | bytes 3145732
  2.5 1.0 %copy-start.1 = (bf16[512,512]{1,0:T(8,128)(2,1)S(1)}, bf16[512,512]{1,0:T(8,128)(2,1)}, u32[]{:S(2)}) copy-start(bf16[512,512]{1,0:T(8,128)(2,1)} %diag.1) | copy-start | bytes 1572868
  3.5 0.9 %copy-start.2 = (f32[64,512]{1,0:T(8,128)S(1)}, f32[64,512]{1,0:T(8,128)}, u32[]{:S(2)}) copy-start(f32[64,512]{1,0:T(8,128)} %hdiag_in.1) | copy-start | bytes 393220
  4.4 0.7 %copy-start.3 = (bf16[64,64]{1,0:T(8,128)(2,1)S(1)}, bf16[64,64]{1,0:T(8,128)(2,1)}, u32[]{:S(2)}) copy-start(bf16[64,64]{1,0:T(8,128)(2,1)} %beta_in.1) | copy-start | bytes 24580
  5.2 0.7 copy-start.4

commit v3 on v2

--- a/solution.py
+++ b/solution.py
@@ -457,7 +457,7 @@
             dma((2,)),
             dma((2,)),
         ],
-        compiler_params=pltpu.CompilerParams(collective_id=0, has_side_effects=True, vmem_limit_bytes=50 * 2**20),
+        compiler_params=pltpu.CompilerParams(collective_id=0, has_side_effects=True),
         name="davidson",
     )(partners, live, trial, coupling, diag_block, beta_coupling, hdiag)
     return correction, subspace[:, : root_count * depth].T

time: 70.1 us -> 68.5 us (0.977)
  local copies, waits for them, and re-layouts: 6.1 us -> 3.58 us
  Pallas kernels: 62.5 us -> 63.4 us
    unnamed x11 -> x1, local copies, waits for them, and re-layouts: 5.5 us -> 2.29 us
    pallas_call x1, Pallas kernels: 62.5 us -> 63.4 us  [exchanged(): pl.pallas_call(functools.partial(kernel, depth), out_shape=(jax.ShapeDtyp...]
where the time goes in v3:
time: 68.5 us; the launch traced here: 68.3 us
  Pallas kernels  63.4 us (93%)
  local copies, waits for them, and re-layouts  3.58 us (5%)
  between operations  1.29 us (2%)
    pallas_call x1, Pallas kernels, exchanged(): pl.pallas_call(functools.partial(kernel, depth), out_shape=(jax.ShapeDtyp...  63.4 us
    unnamed x1, local copies, waits for them, and re-layouts  2.29 us

profile of v3, /device:TPU:0, one launch (start us, length us, event | category | flops | bytes accessed | tf_op | source)
XLA Modules:
  0.0 68.3 jit_solution(12529247356968098270)
XLA Ops:
  1.3 63.4 %davidson.1 = (bf16[16,64,512]{2,1,0:T(8,128)(2,1)}, f32[16,128]{1,0:T(8,128)}) custom-call(s32[1,6]{1,0:T(1,128)} %partners_in.1, s32[1]{0:T(128)S(6)} %copy.10.live, bf16[16,64,512]{2,1,0:T(8,128)(2,1)} %trial.1, bf16[1,6,512,512]{3,2,1,0:T(8,128)(2,1)} %coupling.1, bf16[512,512]{1,0:T(8,128)(2,1)} %diag.1, bf16[64,64]{1,0:T(8,128)(2,1)} %beta_in.1, ...), custom_call_target="tpu_custom_call" | custom-call | tf_op jit(solution)/shard_map/davidson/pallas_call | solution.py:425
  64.7 1.3 %slice_bitcast_fusion = f32[64,16]{0,1:T(8,128)} fusion(f32[16,128]{1,0:T(8,128)} %get-tuple-element.5), kind=kLoop, calls=%fused_computation | loop fusion | bytes 8192 | tf_op jit(solution)/shard_map/transpose | solution.py:463
  66.0 2.3 %copy.11 = bf16[16,64,512]{2,1,0:T(8,128)(2,1)} copy(bf16[16,64,512]{2,1,0:T(8,128)(2,1)} %get-tuple-element.8) | data formatting | bytes 2097152
